TPU v7x, 32 devices: a whole 2x2x4 slice. The times are simulated.
32 devices in a mesh: slab: 4 (over x, core), img: 8 (over z, y).
Axes of the slice: x: 2, y: 2, z: 4, core: 2. Of those that a mesh axis runs over, the one named last changes fastest.
Arguments:
- feats: bfloat16 [8, 32, 128, 512], P('img', 'slab'), may hold values from -6 to 6
- labels: int32 [8], P('img'), may hold values from 0 to 999
- conv_w: bfloat16 [9, 512, 4], replicated, may hold values from -0.09375 to 0.09375
- embed_w: bfloat16 [16, 1024], replicated, may hold values from -1.5 to 1.5
- mod_table: bfloat16 [1000, 2048], replicated, may hold values from -3 to 3
- qkv_w: bfloat16 [1024, 3072], replicated, may hold values from -0.1875 to 0.1875
- out_w: bfloat16 [1024, 1024], replicated, may hold values from -0.1875 to 0.1875
- proj_w: bfloat16 [1024, 768], replicated, may hold values from -0.1875 to 0.1875
- dino: bfloat16 [8, 1024, 768], P('img', 'slab'), may hold values from -6 to 6
Outputs:
- grad_feats: bfloat16 [8, 32, 128, 512], P('img', 'slab')
- grad_proj: float32 [1024, 768], replicated
- grad_conv: float32 [9, 512, 4], replicated
- loss: float32 [], replicated
All inputs are finite; a program needn't handle non-finite values.
Results may differ from a plain program's by a relative error of at most 0.024.
Values may be sent and summed in bfloat16 or wider, within the bound.
A program may use at most 128 MiB of HBM per device.

v0:
```python
import jax
import jax.numpy as jnp
from jax import lax
from jax.sharding import PartitionSpec as P

HEAD_DIM = 64
latent_scale = 0.18215
norm_eps = 1e-06
cosine_eps = 1e-06


def extended(cells, sides, width):
    for axis, dim in sides:
        count = lax.axis_size(axis)
        ends = count - 1
        head = lax.slice_in_dim(cells, 0, width, axis=dim)
        tail = lax.slice_in_dim(cells, cells.shape[dim] - width, cells.shape[dim], axis=dim)
        cells = jnp.concatenate(
            [
                lax.ppermute(tail, axis, [(i, (i + 1) % count) for i in range(ends)]),
                cells,
                lax.ppermute(head, axis, [((i + 1) % count, i) for i in range(ends)]),
            ],
            axis=dim,
        )
    return cells


def conv_out(padded, conv_w):
    rows = padded.shape[0] - 2
    cols = padded.shape[1] - 2
    total = jnp.zeros((rows * cols, conv_w.shape[2]), jnp.float32)
    for tap in range(9):
        view = padded[tap // 3 : tap // 3 + rows, tap % 3 : tap % 3 + cols]
        total = total + jnp.dot(
            view.reshape(rows * cols, -1), conv_w[tap], preferred_element_type=jnp.float32
        )
    return total.reshape(rows, cols, -1) * latent_scale


def contract_first(left, right):
    return lax.dot_general(
        left, right, (((0,), (0,)), ((), ())), preferred_element_type=jnp.float32
    )


def contract_last(left, right):
    return lax.dot_general(
        left, right, (((1,), (1,)), ((), ())), preferred_element_type=jnp.float32
    )


def conv_back(padded, grad_pad, conv_w):
    rows = grad_pad.shape[0] - 2
    cols = grad_pad.shape[1] - 2
    center = grad_pad[1:-1, 1:-1].reshape(rows * cols, -1)
    grad_in = jnp.zeros((rows * cols, conv_w.shape[1]), jnp.float32)
    parts = []
    for tap in range(9):
        row_off = tap // 3
        col_off = tap % 3
        g_view = grad_pad[
            2 - row_off : 2 - row_off + rows, 2 - col_off : 2 - col_off + cols
        ].reshape(rows * cols, -1)
        grad_in = grad_in + contract_last(g_view, conv_w[tap])
        f_view = padded[row_off : row_off + rows, col_off : col_off + cols].reshape(rows * cols, -1)
        parts.append(contract_first(f_view, center))
    return (grad_in.reshape(rows, cols, -1), jnp.stack(parts, 0))


def patchify(latent):
    rows, cols, chans = latent.shape
    blocks = latent.reshape(rows // 2, 2, cols // 2, 2, chans).transpose(0, 2, 1, 3, 4)
    return blocks.reshape(rows // 2 * (cols // 2), 4 * chans)


def unpatchify(tokens, rows, cols):
    chans = tokens.shape[1] // 4
    blocks = tokens.reshape(rows // 2, cols // 2, 2, 2, chans).transpose(0, 2, 1, 3, 4)
    return blocks.reshape(rows, cols, chans)


def cosine_grad(projected, target):
    norm_p = jnp.sqrt(jnp.sum(projected * projected, -1, keepdims=True) + cosine_eps)
    norm_t = jnp.sqrt(jnp.sum(target * target, -1, keepdims=True) + cosine_eps)
    cosine = jnp.sum(projected * target, -1, keepdims=True) / (norm_p * norm_t)
    grad = cosine * projected / (norm_p * norm_p) - target / (norm_p * norm_t)
    return (cosine[:, 0], grad)


def local(feats, labels, conv_w, embed_w, mod_table, qkv_w, out_w, proj_w, dino):
    image = feats[0]
    rows, cols, chans = image.shape
    width = qkv_w.shape[0]
    heads = width // HEAD_DIM
    scale = HEAD_DIM ** (-0.5)
    rimmed = extended(image, (("slab", 0),), 1)
    padded = jnp.pad(rimmed, ((0, 0), (1, 1), (0, 0)))
    tokens = patchify(conv_out(padded, conv_w))
    count = tokens.shape[0]
    embed_f = embed_w.astype(jnp.float32)
    start = jnp.dot(tokens, embed_f, precision=lax.Precision.HIGHEST)
    row = lax.dynamic_index_in_dim(mod_table, labels[0], 0, keepdims=False).astype(jnp.float32)
    mean = jnp.mean(start, -1, keepdims=True)
    cent = start - mean
    inv = lax.rsqrt(jnp.mean(cent * cent, -1, keepdims=True) + norm_eps)
    normed = cent * inv
    modded = (normed * (1.0 + row[width:]) + row[:width]).astype(jnp.bfloat16)
    qkv = jnp.dot(modded, qkv_w, preferred_element_type=jnp.float32).astype(jnp.bfloat16)
    query = qkv[:, :width]
    key = qkv[:, width : 2 * width]
    value = qkv[:, 2 * width :]
    key_all, value_all = (
        lax.all_gather(key, "slab", axis=0, tiled=True),
        lax.all_gather(value, "slab", axis=0, tiled=True),
    )
    q3 = query.reshape(count, heads, HEAD_DIM)
    k3 = key_all.reshape(-1, heads, HEAD_DIM)
    v3 = value_all.reshape(-1, heads, HEAD_DIM)
    scores = jnp.einsum("qhd,khd->hqk", q3, k3, preferred_element_type=jnp.float32) * scale
    top = jnp.max(scores, -1, keepdims=True)
    expo = jnp.exp(scores - top)
    total = jnp.sum(expo, -1)
    attended = (
        jnp.einsum(
            "hqk,khd->qhd", expo.astype(jnp.bfloat16), v3, preferred_element_type=jnp.float32
        )
        / total.T[:, :, None]
    )
    attended = attended.reshape(count, width).astype(jnp.bfloat16)
    lse = top[..., 0] + jnp.log(total)
    resid = start + jnp.dot(attended, out_w, preferred_element_type=jnp.float32)
    resid_b = resid.astype(jnp.bfloat16)
    projected = jnp.dot(resid_b, proj_w, preferred_element_type=jnp.float32)
    cosine, grad_p = cosine_grad(projected, dino[0].astype(jnp.float32))
    grad_pb = grad_p.astype(jnp.bfloat16)
    proj_part = contract_first(resid_b, grad_pb)
    grad_resid = contract_last(grad_pb, proj_w)
    grad_att = contract_last(grad_resid.astype(jnp.bfloat16), out_w).astype(jnp.bfloat16)
    g3 = grad_att.reshape(count, heads, HEAD_DIM)
    delta = jnp.sum(
        g3.astype(jnp.float32) * attended.reshape(count, heads, HEAD_DIM).astype(jnp.float32), -1
    ).T
    probs = jnp.exp(scores - lse[..., None])
    dprobs = jnp.einsum("qhd,khd->hqk", g3, v3, preferred_element_type=jnp.float32)
    dscores = (probs * (dprobs - delta[..., None])).astype(jnp.bfloat16)
    grad_query = scale * jnp.einsum(
        "hqk,khd->qhd", dscores, k3, preferred_element_type=jnp.float32
    ).reshape(count, width)
    key_terms = scale * jnp.einsum(
        "hqk,qhd->khd", dscores, q3, preferred_element_type=jnp.float32
    ).reshape(-1, width)
    value_terms = jnp.einsum(
        "hqk,qhd->khd", probs.astype(jnp.bfloat16), g3, preferred_element_type=jnp.float32
    ).reshape(-1, width)
    grad_key, grad_value = (
        lax.psum_scatter(
            key_terms.astype(jnp.bfloat16), "slab", scatter_dimension=0, tiled=True
        ).astype(jnp.float32),
        lax.psum_scatter(
            value_terms.astype(jnp.bfloat16), "slab", scatter_dimension=0, tiled=True
        ).astype(jnp.float32),
    )
    grad_qkv = jnp.concatenate([grad_query, grad_key, grad_value], 1).astype(jnp.bfloat16)
    grad_mod = contract_last(grad_qkv, qkv_w)
    grad_norm = grad_mod * (1.0 + row[width:])
    grad_start = grad_resid + inv * (
        grad_norm
        - jnp.mean(grad_norm, -1, keepdims=True)
        - normed * jnp.mean(grad_norm * normed, -1, keepdims=True)
    )
    grad_tokens = jnp.dot(grad_start, embed_f.T, precision=lax.Precision.HIGHEST)
    grad_latent = (unpatchify(grad_tokens, rows, cols) * latent_scale).astype(jnp.bfloat16)
    grad_rim = extended(grad_latent, (("slab", 0),), 1)
    grad_pad = jnp.pad(grad_rim, ((0, 0), (1, 1), (0, 0)))
    grad_image, conv_part = conv_back(padded, grad_pad, conv_w)
    loss_part = jnp.sum(1.0 - cosine)
    grad_proj, grad_conv, loss_sum = lax.psum((proj_part, conv_part, loss_part), ("slab", "img"))
    groups = lax.axis_size("slab") * lax.axis_size("img")
    return (
        grad_image.astype(jnp.bfloat16)[None],
        grad_proj,
        grad_conv,
        loss_sum / (groups * count),
    )


def solution(mesh):
    in_specs = (
        P("img", "slab", None, None),
        P("img"),
        P(),
        P(),
        P(),
        P(),
        P(),
        P(),
        P("img", "slab", None),
    )
    out_specs = (P("img", "slab", None, None), P(), P(), P())
    return jax.shard_map(local, mesh=mesh, in_specs=in_specs, out_specs=out_specs, check_vma=False)
```

profile of v0, /device:TPU:0, one launch (start us, length us, event | category | flops | bytes accessed | tf_op | source)
XLA Modules:
  0.0 356.8 jit_solution(18336326718904891435)
XLA Ops:
  8.4 2.4 collective-permute-start
  25.2 1.9 copy.46
  29.6 4.8 %convolution_convert_fusion = bf16[256,3072]{1,0:T(8,128)(2,1)S(1)} fusion(bf16[1024,3072]{1,0:T(8,128)(2,1)} %param.14, f32[256,1024]{1,0:T(8,128)S(1)} %get-tuple-element.33, f32[1024]{0:T(1024)} %bitcast.264, f32[1024]{0:T(1024)S(1)} %bitcast.262, f32[256]{0:T(256)S(1)} %add_rsqrt_fusion, f32[256]{0:T(256)S(1)} %broadcast_multiply_fusion.2), kind=kOutput, calls=%fused_computation.16 | convolution fusion | flops 1612709888 | bytes 8923136 | tf_op jit(solution)/shard_map/dot_general | solution.py:109
  36.4 2.0 copy.48
  38.5 24.5 %all-gather.5.cloned.1.call-done = bf16[1024,1024]{1,0:T(8,128)(2,1)} async-done(((bf16[256,1024]{1,0:T(8,128)(2,1)}), bf16[1024,1024]{1,0:T(8,128)(2,1)}) %all-gather.5.cloned.1.call-update) | async-done | bytes 2097168 | tf_op jit(solution)/shard_map/all_gather | solution.py:114
  63.0 4.0 %copy.49 = bf16[1024,1024]{0,1:T(8,128)(2,1)} copy(bf16[1024,1024]{1,0:T(8,128)(2,1)} %all-gather.5.cloned.1.call-done) | data formatting | bytes 4194304 | tf_op jit(solution)/shard_map/all_gather | solution.py:114
  66.9 4.2 %multiply_reduce_fusion = (f32[16,256]{1,0:T(8,128)S(1)}, f32[16,256,1024]{2,1,0:T(8,128)S(1)}) fusion(bf16[256,16,64]{0,2,1:T(8,128)(2,1)} %bitcast.234, bf16[1024,16,64]{0,2,1:T(8,128)(2,1)} %bitcast.226), kind=kOutput, calls=%fused_computation.6 | convolution fusion | flops 545255424 | bytes 19415040 | tf_op jit(solution)/shard_map/qhd,khd->hqk/dot_general | solution.py:120
  71.2 3.6 %fusion = f32[16,256]{1,0:T(8,128)S(1)} fusion(f32[16,256,1024]{2,1,0:T(8,128)S(1)} %get-tuple-element.35, f32[16,256]{1,0:T(8,128)S(1)} %get-tuple-element.34), kind=kLoop, calls=%fused_computation.3 | loop fusion | flops 12578816 | bytes 16809984 | tf_op jit(solution)/shard_map/reduce_sum | solution.py:123
  74.8 2.3 copy-done.2
  77.9 9.2 %all-gather.3.cloned.1.call-done = bf16[1024,1024]{1,0:T(8,128)(2,1)} async-done(((bf16[256,1024]{1,0:T(8,128)(2,1)}), bf16[1024,1024]{1,0:T(8,128)(2,1)}) %all-gather.3.cloned.1.call-update) | async-done | bytes 2097168 | tf_op jit(solution)/shard_map/all_gather | solution.py:115
  87.1 3.9 %copy.47 = bf16[1024,1024]{0,1:T(8,128)(2,1)} copy(bf16[1024,1024]{1,0:T(8,128)(2,1)} %all-gather.3.cloned.1.call-done) | data formatting | bytes 4194304 | tf_op jit(solution)/shard_map/all_gather | solution.py:115
  91.0 8.3 %divide_convert_fusion = bf16[256,16,64]{0,2,1:T(8,128)(2,1)S(1)} fusion(bf16[1024,16,64]{0,2,1:T(8,128)(2,1)} %bitcast.231, f32[16,256,1024]{2,1,0:T(8,128)} %copy-done.2, f32[16,256]{1,0:T(8,128)} %copy-done.25, f32[256,16]{0,1:T(8,128)} %bitcast.261), kind=kOutput, calls=%fused_computation.83 | convolution fusion | flops 549978112 | bytes 19431424 | tf_op jit(solution)/shard_map/hqk,khd->qhd/dot_general | solution.py:125
  109.0 9.4 %multiply_convert_fusion = bf16[16,256,1024]{2,1,0:T(8,128)(2,1)S(1)} fusion(f32[16,256,1024]{2,1,0:T(8,128)} %copy-done.2, bf16[256,16,64]{0,2,1:T(8,128)(2,1)S(1)} %bitcast.229, bf16[1024,16,64]{0,2,1:T(8,128)(2,1)} %bitcast.232, f32[16,256]{1,0:T(8,128)S(1)} %bitcast.260, f32[16,256]{1,0:T(8,128)S(1)} %log_add_fusion), kind=kOutput, calls=%fused_computation | convolution fusion | flops 557842432 | bytes 27820032 | tf_op jit(solution)/shard_map/qhd,khd->hqk/dot_general | solution.py:145
  118.5 3.4 multiply_convert_fusion.1
  122.4 9.8 %fusion.12 = bf16[16,64,1024]{2,1,0:T(8,128)(2,1)} fusion(bf16[256,16,64]{0,2,1:T(8,128)(2,1)S(1)} %bitcast.230, f32[16,256,1024]{2,1,0:T(8,128)} %copy-done.2, f32[16,256]{1,0:T(8,128)S(1)} %log_add_fusion), kind=kOutput, calls=%fused_computation.19 | convolution fusion | flops 550502400 | bytes 19415040 | tf_op jit(solution)/shard_map/hqk,qhd->khd/dot_general | solution.py:153
  132.3 39.7 %psum.23 = f32[]{:T(128)} all-reduce(f32[]{:T(128)} %get-tuple-element.11), channel_id=1, replica_groups=mesh['slab'=4,'img'=8] {'slab','img'}, use_global_device_ids=true, to_apply=%region_15.16 | all-reduce | flops 1 | bytes 8 | tf_op jit(solution)/shard_map/psum | solution.py:178
  172.7 3.5 fusion.166
  176.3 6.9 %fusion.33 = bf16[16,64,256]{2,1,0:T(8,128)(2,1)} fusion(bf16[1024,16,64]{0,2,1:T(8,128)(2,1)S(1)} %bitcast.227, bf16[16,256,1024]{2,1,0:T(8,128)(2,1)} %copy-done.3), kind=kOutput, calls=%fused_computation.37 | convolution fusion | flops 537395200 | bytes 11010048 | tf_op jit(solution)/shard_map/hqk,khd->qhd/dot_general | solution.py:147
  183.1 4.4 %reduce-scatter.5.cloned.1.call-done = bf16[256,1024]{0,1:T(8,128)(2,1)} async-done(((bf16[1024,1024]{0,1:T(8,128)(2,1)}), bf16[256,1024]{0,1:T(8,128)(2,1)}) %reduce-scatter.5.cloned.1.call-update) | async-done | bytes 524304 | tf_op jit(solution)/shard_map/reduce_scatter | solution.py:160
  187.5 5.7 %fusion.160 = (f32[256]{0:T(256)S(1)}, f32[256]{0:T(256)S(1)}, f32[256,1024]{1,0:T(8,128)S(1)}) fusion(f32[256]{0:T(256)S(1)} %add_rsqrt_fusion, f32[256,1024]{1,0:T(8,128)} %copy-done.7, f32[256]{0:T(256)S(1)} %broadcast_multiply_fusion.2, f32[1024]{0:T(1024)S(1)} %bitcast.263, bf16[1024,3072]{1,0:T(8,128)(2,1)} %param.14, ...), kind=kOutput, calls=%fused_computation.197 | convolution fusion | flops 1616903680 | bytes 9969664 | tf_op jit(solution)/shard_map/dot_general | solution.py:48
  199.0 3.3 collective-permute-start.2
  209.8 2.1 add_convert_fusion
  211.9 132.6 %all-reduce.5.cloned.1.call-done = (f32[1024,768]{1,0:T(8,128)}, f32[9,512,4]{1,2,0:T(4,128)}) async-done(((f32[1024,768]{1,0:T(8,128)}, f32[9,512,4]{1,2,0:T(4,128)}), (f32[1024,768]{1,0:T(8,128)}, f32[9,512,4]{1,2,0:T(4,128)})) %all-reduce.5.cloned.1.call-update) | async-done | bytes 3219472 | tf_op jit(solution)/shard_map/psum | solution.py:178
  344.6 3.9 %copy.88 = f32[1024,768]{1,0:T(8,128)} copy(f32[1024,768]{1,0:T(8,128)} %get-tuple-element.41) | data formatting | bytes 6291456
  (134 shorter events, 44.3 us)
Async XLA Ops:
  7.2 92.2 %copy-start = (bf16[1024,1024]{1,0:T(8,128)(2,1)S(1)}, bf16[1024,1024]{1,0:T(8,128)(2,1)}, u32[]{:S(2)}) copy-start(bf16[1024,1024]{1,0:T(8,128)(2,1)} %param.15) | copy-start | bytes 6291460
  7.2 55.8 %all-gather.5.cloned.1.call-start = ((), (), s32[]{:S(2)}) async-start(), calls=%async_computation.3 | async-start | bytes 2621440 | tf_op jit(solution)/shard_map/all_gather | solution.py:114
  8.4 7.3 %collective-permute-start = (bf16[1,128,512]{2,1,0:T(8,128)(2,1)S(1)}, bf16[1,128,512]{2,1,0:T(8,128)(2,1)S(1)}, u32[]{:S(2)}, u32[]{:S(2)}) collective-permute-start(bf16[1,128,512]{2,1,0:T(8,128)(2,1)S(1)} %get-tuple-element.25), channel_id=1, source_target_pairs={{0,8},{8,16},{16,24},{1,9},{9,17},{17,25},{2,10},{10,18},{18,26},{... | collective-permute-start | bytes 393224 | tf_op jit(solution)/shard_map/ppermute | solution.py:20
  10.8 5.3 %collective-permute-start.1 = (bf16[1,128,512]{2,1,0:T(8,128)(2,1)S(1)}, bf16[1,128,512]{2,1,0:T(8,128)(2,1)S(1)}, u32[]{:S(2)}, u32[]{:S(2)}) collective-permute-start(bf16[1,128,512]{2,1,0:T(8,128)(2,1)S(1)} %get-tuple-element.26), channel_id=1, source_target_pairs={{8,0},{16,8},{24,16},{9,1},{17,9},{25,17},{10,2},{18,10},{26,18},{... | collective-permute-start | bytes 393224 | tf_op jit(solution)/shard_map/ppermute | solution.py:22
  29.3 5.1 %copy-start.7 = (f32[256,1024]{1,0:T(8,128)}, f32[256,1024]{1,0:T(8,128)S(1)}, u32[]{:S(2)}) copy-start(f32[256,1024]{1,0:T(8,128)S(1)} %get-tuple-element.33) | copy-start | bytes 3145732
  35.6 51.5 %all-gather.3.cloned.1.call-start = ((), (), s32[]{:S(2)}) async-start(), calls=%async_computation.2 | async-start | bytes 2621440 | tf_op jit(solution)/shard_map/all_gather | solution.py:115
  36.4 146.7 %reduce-scatter.3.cloned.1.call-start = ((), (), s32[]{:S(2)}) async-start(), calls=%async_computation.4 | async-start | bytes 2621440 | tf_op jit(solution)/shard_map/reduce_scatter | solution.py:157
  71.1 6.0 %copy-start.2 = (f32[16,256,1024]{2,1,0:T(8,128)}, f32[16,256,1024]{2,1,0:T(8,128)S(1)}, u32[]{:S(2)}) copy-start(f32[16,256,1024]{2,1,0:T(8,128)S(1)} %get-tuple-element.35) | copy-start | bytes 50331652
  71.1 6.1 %copy-start.25 = (f32[16,256]{1,0:T(8,128)}, f32[16,256]{1,0:T(8,128)S(1)}, u32[]{:S(2)}) copy-start(f32[16,256]{1,0:T(8,128)S(1)} %get-tuple-element.34) | copy-start | bytes 49156
  91.0 8.3 %copy-start.8 = (f32[256,1024]{1,0:T(8,128)S(1)}, f32[256,1024]{1,0:T(8,128)}, u32[]{:S(2)}) copy-start(f32[256,1024]{1,0:T(8,128)} %copy-done.7) | copy-start | bytes 3145732
  99.4 1.6 copy-start.23
  109.0 9.5 %copy-start.13 = (bf16[256,1024]{0,1:T(8,128)(2,1)S(1)}, bf16[256,1024]{0,1:T(8,128)(2,1)}, u32[]{:S(2)}) copy-start(bf16[256,1024]{0,1:T(8,128)(2,1)} %copy.48) | copy-start | bytes 1572868
  118.5 3.9 %copy-start.3 = (bf16[16,256,1024]{2,1,0:T(8,128)(2,1)}, bf16[16,256,1024]{2,1,0:T(8,128)(2,1)S(1)}, u32[]{:S(2)}) copy-start(bf16[16,256,1024]{2,1,0:T(8,128)(2,1)S(1)} %multiply_convert_fusion) | copy-start | bytes 25165828
  122.4 65.1 %reduce-scatter.5.cloned.1.call-start = ((), (), s32[]{:S(2)}) async-start(), calls=%async_computation.5 | async-start | bytes 2621440 | tf_op jit(solution)/shard_map/reduce_scatter | solution.py:160
  132.3 44.0 %copy-start.6 = (bf16[1024,1024]{0,1:T(8,128)(2,1)S(1)}, bf16[1024,1024]{0,1:T(8,128)(2,1)}, u32[]{:S(2)}) copy-start(bf16[1024,1024]{0,1:T(8,128)(2,1)} %copy.49) | copy-start | bytes 6291460
  132.3 212.3 %all-reduce.5.cloned.1.call-start = ((), (), s32[]{:S(2)}) async-start(), calls=%async_computation.6 | async-start | bytes 6438912 | tf_op jit(solution)/shard_map/psum | solution.py:178
  187.5 5.7 %copy-start.9 = (f32[256,1024]{1,0:T(8,128)S(1)}, f32[256,1024]{1,0:T(8,128)}, u32[]{:S(2)}) copy-start(f32[256,1024]{1,0:T(8,128)} %copy-done.7) | copy-start | bytes 3145732
  187.5 5.7 %copy-start.11 = (f32[256,1024]{1,0:T(8,128)S(1)}, f32[256,1024]{1,0:T(8,128)}, u32[]{:S(2)}) copy-start(f32[256,1024]{1,0:T(8,128)} %copy-done.10) | copy-start | bytes 3145732
  187.5 5.7 %copy-start.26 = (bf16[16,1024]{1,0:T(8,128)(2,1)S(1)}, bf16[16,1024]{1,0:T(8,128)(2,1)}, u32[]{:S(2)}) copy-start(bf16[16,1024]{1,0:T(8,128)(2,1)} %param.12) | copy-start | bytes 98308
  197.4 6.7 %copy-start.20 = (bf16[1,128,512]{2,1,0:T(8,128)(2,1)S(1)}, bf16[1,128,512]{2,1,0:T(8,128)(2,1)}, u32[]{:S(2)}) copy-start(bf16[1,128,512]{2,1,0:T(8,128)(2,1)} %copy-done.18) | copy-start | bytes 393220
  197.6 7.7 %collective-permute-start.3 = (bf16[1,128,4]{2,1,0:T(8,128)(2,1)S(1)}, bf16[1,128,4]{2,1,0:T(8,128)(2,1)S(1)}, u32[]{:S(2)}, u32[]{:S(2)}) collective-permute-start(bf16[1,128,4]{2,1,0:T(8,128)(2,1)S(1)} %get-tuple-element.28), channel_id=1, source_target_pairs={{8,0},{16,8},{24,16},{9,1},{17,9},{25,17},{10,2},{18,10},{26,18},{... | collective-permute-start | bytes 3080 | tf_op jit(solution)/shard_map/ppermute | solution.py:22
  199.0 6.5 %collective-permute-start.2 = (bf16[1,128,4]{2,1,0:T(8,128)(2,1)S(1)}, bf16[1,128,4]{2,1,0:T(8,128)(2,1)S(1)}, u32[]{:S(2)}, u32[]{:S(2)}) collective-permute-start(bf16[1,128,4]{2,1,0:T(8,128)(2,1)S(1)} %get-tuple-element.27), channel_id=1, source_target_pairs={{0,8},{8,16},{16,24},{1,9},{9,17},{17,25},{2,10},{10,18},{18,26},{... | collective-permute-start | bytes 3080 | tf_op jit(solution)/shard_map/ppermute | solution.py:20
  344.6 4.6 %copy-start.1 = (bf16[1024,1024]{1,0:T(8,128)(2,1)S(1)}, bf16[1024,1024]{1,0:T(8,128)(2,1)}, u32[]{:S(2)}) copy-start(bf16[1024,1024]{1,0:T(8,128)(2,1)} %param.15) | copy-start | bytes 6291460
  344.6 3.9 %copy-start.28 = (f32[9,512,4]{1,2,0:T(4,128)S(1)}, f32[9,512,4]{1,2,0:T(4,128)}, u32[]{:S(2)}) copy-start(f32[9,512,4]{1,2,0:T(4,128)} %get-tuple-element.42) | copy-start | bytes 221188
  (15 other events, 16.8 us)
Sparse Core Ops, SparseCore 0:
  35.8 27.1 all-gather.4
  64.5 22.5 all-gather.2
  122.5 31.3 reduce-scatter.2
  156.3 31.1 reduce-scatter.4
  205.5 139.0 all-reduce.4
where the time goes:
time: 358 us; the launch traced here: 357 us
  waiting for transfers between devices  172 us (48%)
  matrix products  78.6 us (22%)
  blocking collectives  39.7 us (11%)
  local copies, waits for them, and re-layouts  32.2 us (9%)
  between operations  16.7 us (5%)
  other arithmetic  9.29 us (3%)
  starting transfers between devices  8.48 us (2%)
    psum x1, waiting for transfers between devices, local(): lax.psum((proj_part, conv_part, loss_part), ('slab', 'img'))  133 us
    psum x1, blocking collectives, local(): lax.psum((proj_part, conv_part, loss_part), ('slab', 'img'))  39.7 us
    all_gather x1, waiting for transfers between devices, local(): lax.all_gather(key, 'slab', axis=0, tiled=True)  24.5 us
    dot_general x12, matrix products, contract_last(): lax.dot_general(left, right, (((1,), (1,)), ((), ())), preferred_element_...  15.3 us
    unnamed x62, local copies, waits for them, and re-layouts  12.8 us
    dot_general x1, matrix products, local(): jnp.einsum('hqk,qhd->khd', probs.astype(jnp.bfloat16), g3, preferred_elem...  9.81 us
    dot_general x1, matrix products, local(): jnp.einsum('qhd,khd->hqk', g3, v3, preferred_element_type=jnp.float32)  9.44 us
    all_gather x1, waiting for transfers between devices, local(): lax.all_gather(value, 'slab', axis=0, tiled=True)  9.23 us
  transfers between devices with their start and end apart: 9, of which 5 were waited for; matrix products, arithmetic and copies ran while one was open for 13% of the time, Pallas kernels for 0%

commit v1 on v0

--- a/solution.py
+++ b/solution.py
@@ -89,6 +89,12 @@
 
 
 def local(feats, labels, conv_w, embed_w, mod_table, qkv_w, out_w, proj_w, dino):
+
+    def keep_up_hubs(vals, bus_axis, mesh_ax):
+        for pp in (bus_axis, mesh_ax):
+            vals = lax.psum(vals, pp)
+        return vals
+
     image = feats[0]
     rows, cols, chans = image.shape
     width = qkv_w.shape[0]
@@ -175,7 +181,7 @@
     grad_pad = jnp.pad(grad_rim, ((0, 0), (1, 1), (0, 0)))
     grad_image, conv_part = conv_back(padded, grad_pad, conv_w)
     loss_part = jnp.sum(1.0 - cosine)
-    grad_proj, grad_conv, loss_sum = lax.psum((proj_part, conv_part, loss_part), ("slab", "img"))
+    grad_proj, grad_conv, loss_sum = keep_up_hubs((proj_part, conv_part, loss_part), "img", "slab")
     groups = lax.axis_size("slab") * lax.axis_size("img")
     return (
         grad_image.astype(jnp.bfloat16)[None],

time: 358 us -> 415 us (1.16)
  waiting for transfers between devices: 172 us -> 234 us
  blocking collectives: 39.7 us -> 29.8 us
    reduce_scatter x1, waiting for transfers between devices: 4.35 us -> 33.6 us  [local(): lax.psum_scatter(value_terms.astype(jnp.bfloat16), 'slab', scatter_dimens...]
    psum x1 -> x2, waiting for transfers between devices: 133 us -> 154 us  [keep_up_hubs(): vals = lax.psum(vals, pp)]
    reduce_scatter x1, waiting for transfers between devices: 0.01 us -> 10.9 us  [local(): lax.psum_scatter(key_terms.astype(jnp.bfloat16), 'slab', scatter_dimensio...]
    psum x1 -> x2, blocking collectives: 39.7 us -> 29.8 us  [keep_up_hubs(): vals = lax.psum(vals, pp)]
    unnamed x62 -> x70, local copies, waits for them, and re-layouts: 12.8 us -> 13.9 us
  transfers between devices with their start and end apart: 9 -> 10, of which waited for: 5 -> 7; matrix products, arithmetic and copies ran while one was open for 13% -> 12% of each run, Pallas kernels for 0% -> 0%
where the time goes in v1:
time: 415 us; the launch traced here: 414 us
  waiting for transfers between devices  234 us (56%)
  matrix products  82.3 us (20%)
  local copies, waits for them, and re-layouts  33.3 us (8%)
  blocking collectives  29.8 us (7%)
  between operations  17 us (4%)
  other arithmetic  9.29 us (2%)
  starting transfers between devices  8.65 us (2%)
    psum x2, waiting for transfers between devices, keep_up_hubs(): vals = lax.psum(vals, pp)  154 us
    reduce_scatter x1, waiting for transfers between devices, local(): lax.psum_scatter(value_terms.astype(jnp.bfloat16), 'slab', scatter_dimens...  33.6 us
    psum x2, blocking collectives, keep_up_hubs(): vals = lax.psum(vals, pp)  29.8 us
    all_gather x1, waiting for transfers between devices, local(): lax.all_gather(key, 'slab', axis=0, tiled=True)  24.5 us
    dot_general x12, matrix products, contract_last(): lax.dot_general(left, right, (((1,), (1,)), ((), ())), preferred_element_...  19 us
    unnamed x70, local copies, waits for them, and re-layouts  13.9 us
    reduce_scatter x1, waiting for transfers between devices, local(): lax.psum_scatter(key_terms.astype(jnp.bfloat16), 'slab', scatter_dimensio...  10.9 us
    dot_general x1, matrix products, local(): jnp.einsum('hqk,qhd->khd', probs.astype(jnp.bfloat16), g3, preferred_elem...  9.81 us
  transfers between devices with their start and end apart: 10, of which 7 were waited for; matrix products, arithmetic and copies ran while one was open for 12% of the time, Pallas kernels for 0%

profile of v1, /device:TPU:0, one launch (start us, length us, event | category | flops | bytes accessed | tf_op | source)
XLA Modules:
  0.0 414.1 jit_solution(851235638440522062)
XLA Ops:
  8.4 2.4 collective-permute-start
  29.6 4.8 %convolution_convert_fusion = bf16[256,3072]{1,0:T(8,128)(2,1)S(1)} fusion(bf16[1024,3072]{1,0:T(8,128)(2,1)} %param.14, f32[256,1024]{1,0:T(8,128)S(1)} %get-tuple-element.35, f32[1024]{0:T(1024)} %bitcast.264, f32[1024]{0:T(1024)S(1)} %bitcast.262, f32[256]{0:T(256)S(1)} %add_rsqrt_fusion, f32[256]{0:T(256)S(1)} %broadcast_multiply_fusion.2), kind=kOutput, calls=%fused_computation.16 | convolution fusion | flops 1612709888 | bytes 8923136 | tf_op jit(solution)/shard_map/dot_general | solution.py:115
  38.5 24.5 %all-gather.5.cloned.1.call-done = bf16[1024,1024]{1,0:T(8,128)(2,1)} async-done(((bf16[256,1024]{1,0:T(8,128)(2,1)}), bf16[1024,1024]{1,0:T(8,128)(2,1)}) %all-gather.5.cloned.1.call-update) | async-done | bytes 2097168 | tf_op jit(solution)/shard_map/all_gather | solution.py:120
  62.9 4.0 copy.49
  66.9 4.2 %multiply_reduce_fusion = (f32[16,256]{1,0:T(8,128)S(1)}, f32[16,256,1024]{2,1,0:T(8,128)S(1)}) fusion(bf16[256,16,64]{0,2,1:T(8,128)(2,1)} %bitcast.234, bf16[1024,16,64]{0,2,1:T(8,128)(2,1)} %bitcast.226), kind=kOutput, calls=%fused_computation.6 | convolution fusion | flops 545255424 | bytes 19415040 | tf_op jit(solution)/shard_map/qhd,khd->hqk/dot_general | solution.py:126
  71.1 3.6 fusion
  74.8 2.3 copy-done.2
  77.9 9.2 %all-gather.3.cloned.1.call-done = bf16[1024,1024]{1,0:T(8,128)(2,1)} async-done(((bf16[256,1024]{1,0:T(8,128)(2,1)}), bf16[1024,1024]{1,0:T(8,128)(2,1)}) %all-gather.3.cloned.1.call-update) | async-done | bytes 2097168 | tf_op jit(solution)/shard_map/all_gather | solution.py:121
  87.1 3.9 copy.47
  91.0 8.3 %divide_convert_fusion = bf16[256,16,64]{0,2,1:T(8,128)(2,1)S(1)} fusion(bf16[1024,16,64]{0,2,1:T(8,128)(2,1)} %bitcast.231, f32[16,256,1024]{2,1,0:T(8,128)} %copy-done.2, f32[16,256]{1,0:T(8,128)} %copy-done.29, f32[256,16]{0,1:T(8,128)} %bitcast.261), kind=kOutput, calls=%fused_computation.83 | convolution fusion | flops 549978112 | bytes 19431424 | tf_op jit(solution)/shard_map/hqk,khd->qhd/dot_general | solution.py:131
  109.0 9.4 %multiply_convert_fusion = bf16[16,256,1024]{2,1,0:T(8,128)(2,1)S(1)} fusion(f32[16,256,1024]{2,1,0:T(8,128)} %copy-done.2, bf16[256,16,64]{0,2,1:T(8,128)(2,1)S(1)} %bitcast.229, bf16[1024,16,64]{0,2,1:T(8,128)(2,1)} %bitcast.232, f32[16,256]{1,0:T(8,128)S(1)} %bitcast.260, f32[16,256]{1,0:T(8,128)S(1)} %log_add_fusion), kind=kOutput, calls=%fused_computation | convolution fusion | flops 557842432 | bytes 27820032 | tf_op jit(solution)/shard_map/qhd,khd->hqk/dot_general | solution.py:151
  118.4 3.4 multiply_convert_fusion.1
  122.4 9.8 %fusion.12 = bf16[16,64,1024]{2,1,0:T(8,128)(2,1)} fusion(bf16[256,16,64]{0,2,1:T(8,128)(2,1)S(1)} %bitcast.230, f32[16,256,1024]{2,1,0:T(8,128)} %copy-done.2, f32[16,256]{1,0:T(8,128)S(1)} %log_add_fusion), kind=kOutput, calls=%fused_computation.19 | convolution fusion | flops 550502400 | bytes 19415040 | tf_op jit(solution)/shard_map/hqk,qhd->khd/dot_general | solution.py:159
  132.3 3.6 fusion.166
  135.9 6.9 %fusion.33 = bf16[16,64,256]{2,1,0:T(8,128)(2,1)} fusion(bf16[1024,16,64]{0,2,1:T(8,128)(2,1)S(1)} %bitcast.227, bf16[16,256,1024]{2,1,0:T(8,128)(2,1)} %copy-done.3), kind=kOutput, calls=%fused_computation.37 | convolution fusion | flops 537395200 | bytes 11010048 | tf_op jit(solution)/shard_map/hqk,khd->qhd/dot_general | solution.py:153
  142.7 10.9 %reduce-scatter.3.cloned.1.call-done = bf16[256,1024]{0,1:T(8,128)(2,1)} async-done(((bf16[1024,1024]{0,1:T(8,128)(2,1)}), bf16[256,1024]{0,1:T(8,128)(2,1)}) %reduce-scatter.3.cloned.1.call-update) | async-done | bytes 524304 | tf_op jit(solution)/shard_map/reduce_scatter | solution.py:163
  153.7 33.6 %reduce-scatter.5.cloned.1.call-done = bf16[256,1024]{0,1:T(8,128)(2,1)} async-done(((bf16[1024,1024]{0,1:T(8,128)(2,1)}), bf16[256,1024]{0,1:T(8,128)(2,1)}) %reduce-scatter.5.cloned.1.call-update) | async-done | bytes 524304 | tf_op jit(solution)/shard_map/reduce_scatter | solution.py:166
  187.3 5.7 %fusion.160 = (f32[256]{0:T(256)S(1)}, f32[256]{0:T(256)S(1)}, f32[256,1024]{1,0:T(8,128)S(1)}) fusion(f32[256]{0:T(256)S(1)} %add_rsqrt_fusion, f32[256,1024]{1,0:T(8,128)} %copy-done.7, f32[256]{0:T(256)S(1)} %broadcast_multiply_fusion.2, f32[1024]{0:T(1024)S(1)} %bitcast.263, bf16[1024,3072]{1,0:T(8,128)(2,1)} %param.14, ...), kind=kOutput, calls=%fused_computation.197 | convolution fusion | flops 1616903680 | bytes 9969664 | tf_op jit(solution)/shard_map/dot_general | solution.py:48
  199.1 23.1 %psum.46 = f32[]{:T(128)} all-reduce(f32[]{:T(128)} %get-tuple-element.13), channel_id=1, replica_groups=mesh['slab'=4,'img'=8] {'img'}, use_global_device_ids=true, to_apply=%region_17.18 | all-reduce | flops 1 | bytes 8 | tf_op jit(solution)/shard_map/psum | solution.py:95
  222.1 6.7 %psum.47 = f32[]{:T(128)} all-reduce(f32[]{:T(128)} %psum.46), channel_id=1, replica_groups=mesh['slab'=4,'img'=8] {'slab'}, use_global_device_ids=true, to_apply=%region_18.19 | all-reduce | flops 1 | bytes 8 | tf_op jit(solution)/shard_map/psum | solution.py:95
  231.0 3.3 collective-permute-start.2
  241.7 88.6 %all-reduce.7.cloned.1.call-done = (f32[1024,768]{1,0:T(8,128)}, f32[9,512,4]{1,2,0:T(4,128)}) async-done(((f32[1024,768]{1,0:T(8,128)}, f32[9,512,4]{1,2,0:T(4,128)}), (f32[1024,768]{1,0:T(8,128)}, f32[9,512,4]{1,2,0:T(4,128)})) %all-reduce.7.cloned.1.call-update) | async-done | bytes 3219472 | tf_op jit(solution)/shard_map/psum | solution.py:95
  335.9 65.6 %all-reduce.9.cloned.1.call-done = (f32[1024,768]{1,0:T(8,128)}, f32[9,512,4]{1,2,0:T(4,128)}) async-done(((f32[1024,768]{1,0:T(8,128)}, f32[9,512,4]{1,2,0:T(4,128)}), (f32[1024,768]{1,0:T(8,128)}, f32[9,512,4]{1,2,0:T(4,128)})) %all-reduce.9.cloned.1.call-update) | async-done | bytes 3219472 | tf_op jit(solution)/shard_map/psum | solution.py:95
  401.5 3.9 copy.90
  (146 shorter events, 55.3 us)
Async XLA Ops:
  7.2 92.2 %copy-start = (bf16[1024,1024]{1,0:T(8,128)(2,1)S(1)}, bf16[1024,1024]{1,0:T(8,128)(2,1)}, u32[]{:S(2)}) copy-start(bf16[1024,1024]{1,0:T(8,128)(2,1)} %param.15) | copy-start | bytes 6291460
  7.2 55.8 %all-gather.5.cloned.1.call-start = ((), (), s32[]{:S(2)}) async-start(), calls=%async_computation.3 | async-start | bytes 2621440 | tf_op jit(solution)/shard_map/all_gather | solution.py:120
  8.4 7.3 %collective-permute-start = (bf16[1,128,512]{2,1,0:T(8,128)(2,1)S(1)}, bf16[1,128,512]{2,1,0:T(8,128)(2,1)S(1)}, u32[]{:S(2)}, u32[]{:S(2)}) collective-permute-start(bf16[1,128,512]{2,1,0:T(8,128)(2,1)S(1)} %get-tuple-element.27), channel_id=1, source_target_pairs={{0,8},{8,16},{16,24},{1,9},{9,17},{17,25},{2,10},{10,18},{18,26},{... | collective-permute-start | bytes 393224 | tf_op jit(solution)/shard_map/ppermute | solution.py:20
  10.8 5.3 %collective-permute-start.1 = (bf16[1,128,512]{2,1,0:T(8,128)(2,1)S(1)}, bf16[1,128,512]{2,1,0:T(8,128)(2,1)S(1)}, u32[]{:S(2)}, u32[]{:S(2)}) collective-permute-start(bf16[1,128,512]{2,1,0:T(8,128)(2,1)S(1)} %get-tuple-element.28), channel_id=1, source_target_pairs={{8,0},{16,8},{24,16},{9,1},{17,9},{25,17},{10,2},{18,10},{26,18},{... | collective-permute-start | bytes 393224 | tf_op jit(solution)/shard_map/ppermute | solution.py:22
  29.3 5.1 %copy-start.7 = (f32[256,1024]{1,0:T(8,128)}, f32[256,1024]{1,0:T(8,128)S(1)}, u32[]{:S(2)}) copy-start(f32[256,1024]{1,0:T(8,128)S(1)} %get-tuple-element.35) | copy-start | bytes 3145732
  35.6 51.5 %all-gather.3.cloned.1.call-start = ((), (), s32[]{:S(2)}) async-start(), calls=%async_computation.2 | async-start | bytes 2621440 | tf_op jit(solution)/shard_map/all_gather | solution.py:121
  36.4 117.3 %reduce-scatter.3.cloned.1.call-start = ((), (), s32[]{:S(2)}) async-start(), calls=%async_computation.4 | async-start | bytes 2621440 | tf_op jit(solution)/shard_map/reduce_scatter | solution.py:163
  71.1 6.0 %copy-start.2 = (f32[16,256,1024]{2,1,0:T(8,128)}, f32[16,256,1024]{2,1,0:T(8,128)S(1)}, u32[]{:S(2)}) copy-start(f32[16,256,1024]{2,1,0:T(8,128)S(1)} %get-tuple-element.37) | copy-start | bytes 50331652
  71.1 6.1 %copy-start.29 = (f32[16,256]{1,0:T(8,128)}, f32[16,256]{1,0:T(8,128)S(1)}, u32[]{:S(2)}) copy-start(f32[16,256]{1,0:T(8,128)S(1)} %get-tuple-element.36) | copy-start | bytes 49156
  91.0 8.3 %copy-start.8 = (f32[256,1024]{1,0:T(8,128)S(1)}, f32[256,1024]{1,0:T(8,128)}, u32[]{:S(2)}) copy-start(f32[256,1024]{1,0:T(8,128)} %copy-done.7) | copy-start | bytes 3145732
  109.0 9.5 %copy-start.15 = (bf16[256,1024]{0,1:T(8,128)(2,1)S(1)}, bf16[256,1024]{0,1:T(8,128)(2,1)}, u32[]{:S(2)}) copy-start(bf16[256,1024]{0,1:T(8,128)(2,1)} %copy.48) | copy-start | bytes 1572868
  118.4 3.9 copy-start.3
  122.3 64.9 %reduce-scatter.5.cloned.1.call-start = ((), (), s32[]{:S(2)}) async-start(), calls=%async_computation.5 | async-start | bytes 2621440 | tf_op jit(solution)/shard_map/reduce_scatter | solution.py:166
  132.2 198.0 %all-reduce.7.cloned.1.call-start = ((), (), s32[]{:S(2)}) async-start(), calls=%async_computation.6 | async-start | bytes 6438912 | tf_op jit(solution)/shard_map/psum | solution.py:95
  187.3 5.7 %copy-start.9 = (f32[256,1024]{1,0:T(8,128)S(1)}, f32[256,1024]{1,0:T(8,128)}, u32[]{:S(2)}) copy-start(f32[256,1024]{1,0:T(8,128)} %copy-done.7) | copy-start | bytes 3145732
  187.3 5.7 %copy-start.11 = (f32[256,1024]{1,0:T(8,128)S(1)}, f32[256,1024]{1,0:T(8,128)}, u32[]{:S(2)}) copy-start(f32[256,1024]{1,0:T(8,128)} %copy-done.10) | copy-start | bytes 3145732
  187.3 5.7 %copy-start.30 = (bf16[16,1024]{1,0:T(8,128)(2,1)S(1)}, bf16[16,1024]{1,0:T(8,128)(2,1)}, u32[]{:S(2)}) copy-start(bf16[16,1024]{1,0:T(8,128)(2,1)} %param.12) | copy-start | bytes 98308
  194.3 35.2 %copy-start.16 = (bf16[4,64,2,2,4]{4,3,1,2,0:T(2,128)(2,1)}, bf16[4,64,2,2,4]{4,3,1,2,0:T(2,128)(2,1)S(1)}, u32[]{:S(2)}) copy-start(bf16[4,64,2,2,4]{4,3,1,2,0:T(2,128)(2,1)S(1)} %copy.51) | copy-start | bytes 24580
  199.0 202.5 %all-reduce.9.cloned.1.call-start = ((), (), s32[]{:S(2)}) async-start(), calls=%async_computation.7 | async-start | bytes 6438912 | tf_op jit(solution)/shard_map/psum | solution.py:95
  229.5 6.1 %copy-start.17 = (bf16[4,64,2,2,4]{4,3,1,2,0:T(2,128)(2,1)S(1)}, bf16[4,64,2,2,4]{4,3,1,2,0:T(2,128)(2,1)}, u32[]{:S(2)}) copy-start(bf16[4,64,2,2,4]{4,3,1,2,0:T(2,128)(2,1)} %copy-done.16) | copy-start | bytes 24580
  229.5 6.2 %collective-permute-start.3 = (bf16[1,128,4]{2,1,0:T(8,128)(2,1)S(1)}, bf16[1,128,4]{2,1,0:T(8,128)(2,1)S(1)}, u32[]{:S(2)}, u32[]{:S(2)}) collective-permute-start(bf16[1,128,4]{2,1,0:T(8,128)(2,1)S(1)} %get-tuple-element.30), channel_id=1, source_target_pairs={{8,0},{16,8},{24,16},{9,1},{17,9},{25,17},{10,2},{18,10},{26,18},{... | collective-permute-start | bytes 3080 | tf_op jit(solution)/shard_map/ppermute | solution.py:22
  231.0 4.9 %collective-permute-start.2 = (bf16[1,128,4]{2,1,0:T(8,128)(2,1)S(1)}, bf16[1,128,4]{2,1,0:T(8,128)(2,1)S(1)}, u32[]{:S(2)}, u32[]{:S(2)}) collective-permute-start(bf16[1,128,4]{2,1,0:T(8,128)(2,1)S(1)} %get-tuple-element.29), channel_id=1, source_target_pairs={{0,8},{8,16},{16,24},{1,9},{9,17},{17,25},{2,10},{10,18},{18,26},{... | collective-permute-start | bytes 3080 | tf_op jit(solution)/shard_map/ppermute | solution.py:20
  401.5 4.6 %copy-start.1 = (bf16[1024,1024]{1,0:T(8,128)(2,1)S(1)}, bf16[1024,1024]{1,0:T(8,128)(2,1)}, u32[]{:S(2)}) copy-start(bf16[1024,1024]{1,0:T(8,128)(2,1)} %param.15) | copy-start | bytes 6291460
  401.5 3.9 copy-start.32
  (20 other events, 27.2 us)
Sparse Core Ops, SparseCore 0:
  35.7 27.1 all-gather.4
  64.5 22.5 all-gather.2
  122.5 31.1 reduce-scatter.2
  156.1 31.1 reduce-scatter.4
  199.1 131.1 all-reduce.6
  332.6 68.9 all-reduce.8
